TPU v7x, 32 devices: a whole 2x2x4 slice. The times are simulated.
32 devices in a mesh: seq: 8 (over z, y), head: 4 (over x, core).
Axes of the slice: x: 2, y: 2, z: 4, core: 2. Of those that a mesh axis runs over, the one named last changes fastest.
Arguments:
- queries: bfloat16 [4096, 4096], P('seq', 'head'), may hold values from -5 to 5
- keys: bfloat16 [4096, 1024], P('seq', 'head'), may hold values from -5 to 5
- values: bfloat16 [4096, 1024], P('seq', 'head'), may hold values from -5 to 5
- doc_lengths: int32 [16], replicated, may hold values from 1 to 2048, 4096 in all
- out_weight: bfloat16 [4096, 4096], P('head', 'seq'), may hold values from -0.125 to 0.125
Outputs:
- mixed: bfloat16 [4096, 4096], P('seq', 'head')
Inputs may be any that keep to these rules, and one draw needn't show every extreme that they name: `doc_lengths`: the lengths sum to 4096, and one document is exactly 2048 tokens long.
All inputs are finite; a program needn't handle non-finite values.
Results may differ from a plain program's by a relative error of at most 0.012.
Values may be sent and summed in bfloat16 or wider, within the bound.
A program may use at most 128 MiB of HBM per device.

v0:
```python
import math
import jax
import jax.numpy as jnp
from jax import lax
from jax.sharding import PartitionSpec as P

HQ = 32
KV = 8
DH = 128
REACH = 4


def from_behind(block, axis, distance):
    devices = range(lax.axis_size(axis))
    route = [(i - distance, i) for i in devices if i - distance in devices]
    return lax.ppermute(block, axis, route)


def doc_index(positions, starts):
    return jnp.sum((starts[None, :] <= positions[:, None]).astype(jnp.int32), axis=1) - 1


def body(queries, keys, values, doc_lengths, out_weight):
    local_rows = queries.shape[0]
    kv_local = keys.shape[1] // DH
    group_size = HQ // KV
    temper = DH ** (-0.5)
    starts = jnp.cumsum(doc_lengths) - doc_lengths
    q_first = lax.axis_index("seq") * local_rows
    q_pos = q_first + jnp.arange(local_rows, dtype=jnp.int32)
    q_doc = doc_index(q_pos, starts)
    q_heads = queries.reshape(local_rows, kv_local, group_size, DH)

    def attend(carry, piece, piece_start):
        key_piece, value_piece = piece
        key_count = key_piece.shape[0]
        block_len = math.gcd(key_count, 512)
        num_blocks = key_count // block_len
        key_blocks = key_piece.reshape(num_blocks, block_len, kv_local, DH)
        value_blocks = value_piece.reshape(num_blocks, block_len, kv_local, DH)
        block_starts = piece_start + block_len * jnp.arange(num_blocks, dtype=jnp.int32)

        def one_block(state, entry):
            key_block, value_block, block_first = entry
            k_pos = block_first + jnp.arange(block_len, dtype=jnp.int32)
            k_doc = doc_index(k_pos, starts)
            needed = (block_first >= 0) & (block_first <= q_pos[-1]) & (k_doc[-1] >= q_doc[0])

            def update(inner):
                row_max, row_sum, accum = inner
                scores = (
                    jnp.einsum(
                        "qkgd,nkd->kgqn", q_heads, key_block, preferred_element_type=jnp.float32
                    )
                    * temper
                )
                allowed = (k_doc[None, :] == q_doc[:, None]) & (k_pos[None, :] <= q_pos[:, None])
                scores = jnp.where(allowed[None, None], scores, jnp.float32(-1e30))
                new_max = jnp.maximum(row_max, jnp.max(scores, axis=-1))
                probs = jnp.where(
                    allowed[None, None], jnp.exp(scores - new_max[..., None]), jnp.float32(0.0)
                )
                fading = jnp.exp(row_max - new_max)
                row_sum = row_sum * fading + jnp.sum(probs, axis=-1)
                weights = probs.astype(jnp.bfloat16)
                accum = accum * fading[..., None] + jnp.einsum(
                    "kgqn,nkd->kgqd", weights, value_block, preferred_element_type=jnp.float32
                )
                return (new_max, row_sum, accum)

            def unchanged(inner):
                return inner

            return (lax.cond(needed, update, unchanged, state), None)

        carry, _ = lax.scan(one_block, carry, (key_blocks, value_blocks, block_starts))
        return carry

    initial = (
        jnp.full((kv_local, group_size, local_rows), -1e30, jnp.float32),
        jnp.zeros((kv_local, group_size, local_rows), jnp.float32),
        jnp.zeros((kv_local, group_size, local_rows, DH), jnp.float32),
    )
    final = attend(initial, (keys, values), q_first)
    paired = jnp.stack((keys, values))
    for offset in range(REACH):
        paired = from_behind(paired, "seq", 1)
        final = attend(final, (paired[0], paired[1]), q_first - (offset + 1) * local_rows)
    row_max, row_sum, accum = final
    attn = (accum / row_sum[..., None]).astype(jnp.bfloat16)
    attn = jnp.transpose(attn, (2, 0, 1, 3)).reshape(local_rows, kv_local * group_size * DH)
    partial_terms = jnp.dot(
        attn,
        lax.all_gather(out_weight, "seq", axis=1, tiled=True),
        preferred_element_type=jnp.float32,
    )
    return lax.psum_scatter(
        partial_terms.astype(jnp.bfloat16), "head", scatter_dimension=1, tiled=True
    )


def solution(mesh):
    return jax.shard_map(
        body,
        mesh=mesh,
        in_specs=(P("seq", "head"), P("seq", "head"), P("seq", "head"), P(), P("head", "seq")),
        out_specs=P("seq", "head"),
        check_vma=False,
    )
```

profile of v0, /device:TPU:0, one launch (start us, length us, event | category | flops | bytes accessed | tf_op | source)
XLA Modules:
  0.0 233.1 jit_solution(17083058643937626783)
XLA Ops:
  6.5 0.7 all-gather.2.cloned.1.call-update
  7.3 1.1 copy.53
  8.4 1.1 copy.55
  9.6 4.9 %collective-permute-start = (bf16[2,512,256]{1,2,0:T(8,128)(2,1)S(1)}, bf16[2,512,256]{1,2,0:T(8,128)(2,1)S(1)}, u32[]{:S(2)}, u32[]{:S(2)}) collective-permute-start(bf16[2,512,256]{1,2,0:T(8,128)(2,1)S(1)} %pad_maximum_fusion), channel_id=1, source_target_pairs={{0,4},{4,8},{8,12},{12,16},{16,20},{20,24},{24,28},{1,5},{5,9},{9,... | collective-permute-start | bytes 1572872 | tf_op jit(solution)/shard_map/ppermute | solution.py:16
  14.5 0.7 copy.52
  15.4 0.7 sub.95
  16.1 15.3 %collective-permute-done = bf16[2,512,256]{1,2,0:T(8,128)(2,1)S(1)} collective-permute-done((bf16[2,512,256]{1,2,0:T(8,128)(2,1)S(1)}, bf16[2,512,256]{1,2,0:T(8,128)(2,1)S(1)}, u32[]{:S(2)}, u32[]{:S(2)}) %collective-permute-start) | collective-permute-done | bytes 524320 | tf_op jit(solution)/shard_map/ppermute | solution.py:16
  31.4 4.4 %collective-permute-start.1 = (bf16[2,512,256]{1,2,0:T(8,128)(2,1)S(1)}, bf16[2,512,256]{1,2,0:T(8,128)(2,1)S(1)}, u32[]{:S(2)}, u32[]{:S(2)}) collective-permute-start(bf16[2,512,256]{1,2,0:T(8,128)(2,1)S(1)} %collective-permute-done), channel_id=1, source_target_pairs={{0,4},{4,8},{8,12},{12,16},{16,20},{20,24},{24,28},{1,5},{5,9},{9,... | collective-permute-start | bytes 1572872 | tf_op jit(solution)/shard_map/ppermute | solution.py:16
  36.0 12.2 %collective-permute-done.1 = bf16[2,512,256]{1,2,0:T(8,128)(2,1)S(1)} collective-permute-done((bf16[2,512,256]{1,2,0:T(8,128)(2,1)S(1)}, bf16[2,512,256]{1,2,0:T(8,128)(2,1)S(1)}, u32[]{:S(2)}, u32[]{:S(2)}) %collective-permute-start.1) | collective-permute-done | bytes 524320 | tf_op jit(solution)/shard_map/ppermute | solution.py:16
  48.1 12.2 %collective-permute-start.2 = (bf16[2,512,256]{1,2,0:T(8,128)(2,1)S(1)}, bf16[2,512,256]{1,2,0:T(8,128)(2,1)}, u32[]{:S(2)}, u32[]{:S(2)}) collective-permute-start(bf16[2,512,256]{1,2,0:T(8,128)(2,1)S(1)} %collective-permute-done.1), channel_id=1, source_target_pairs={{0,4},{4,8},{8,12},{12,16},{16,20},{20,24},{24,28},{1,5},{5,9},{9,... | collective-permute-start | bytes 1572872 | tf_op jit(solution)/shard_map/ppermute | solution.py:16
  60.3 6.6 %collective-permute-done.2 = bf16[2,512,256]{1,2,0:T(8,128)(2,1)} collective-permute-done((bf16[2,512,256]{1,2,0:T(8,128)(2,1)S(1)}, bf16[2,512,256]{1,2,0:T(8,128)(2,1)}, u32[]{:S(2)}, u32[]{:S(2)}) %collective-permute-start.2) | collective-permute-done | bytes 524320 | tf_op jit(solution)/shard_map/ppermute | solution.py:16
  66.9 19.1 %collective-permute-start.3 = (bf16[2,512,256]{1,2,0:T(8,128)(2,1)}, bf16[2,512,256]{1,2,0:T(8,128)(2,1)}, u32[]{:S(2)}, u32[]{:S(2)}) collective-permute-start(bf16[2,512,256]{1,2,0:T(8,128)(2,1)} %collective-permute-done.2), channel_id=1, source_target_pairs={{0,4},{4,8},{8,12},{12,16},{16,20},{20,24},{24,28},{1,5},{5,9},{9,... | collective-permute-start | bytes 1572872 | tf_op jit(solution)/shard_map/ppermute | solution.py:16
  86.1 0.6 fusion.68
  86.7 0.6 slice.72
  90.4 0.6 slice.73
  92.2 0.6 slice.75
  93.9 0.7 slice.76
  95.8 0.6 slice.77
  98.7 1.5 copy.54
  100.4 7.7 %conditional.5 = ((f32[2,4,512]{2,1,0:T(4,128)S(1)}, f32[2,4,512]{2,1,0:T(4,128)S(1)}, f32[2,4,512,128]{3,2,1,0:T(8,128)S(1)})) conditional(s32[]{:T(128)} %convert_element_type.72, (f32[2,4,512]{2,1,0:T(4,128)S(1)}, f32[2,4,512]{2,1,0:T(4,128)S(1)}, f32[2,4,512,128]{3,2,1,0:T(8,128)S(1)}) %tuple.52, (s32[512]{0:T(512)S(1)}, s32[512]{0:T(512)S(1)}, ...), branch_computations={%region_6.7_spmd, %region_7.10_spmd} | conditional | flops 1102848000 | bytes 33296444 | solution.py:74
  100.4 0.3 compare_and_fusion
  100.7 1.6 fusion
  102.4 2.0 fusion.2
  104.5 3.6 %multiply_add_fusion = f32[2,4,512,128]{3,2,1,0:T(8,128)S(1)} fusion(f32[2,4,512,128]{3,2,1,0:T(8,128)S(1)} %get-tuple-element.301, f32[2,512,512,4]{2,1,3,0:T(8,128)S(1)} %get-tuple-element.540, f32[2,4,512]{2,1,0:T(4,128)S(1)} %max.11, pred[512,512]{0,1:T(8,128)(4,1)S(1)} %compare_and_fusion, f32[2,4,512]{2,1,0:T(4,128)S(1)} %bitcast.225, ...), kind=kOutput, calls=%fused_computation.7 | convolution fusion | flops 548405248 | bytes 13139968 | tf_op jit(solution)/shard_map/while/body/eval_jaxpr/cond/branch_1_fun/kgqn,nkd->kgqd/dot_general | solution.py:66
  108.1 1.1 fusion.67
  109.4 1.1 fusion.66
  110.7 1.8 conditional.9
  110.8 1.8 copy.110
  112.6 1.9 divide_convert_fusion
  114.5 53.9 %all-gather.2.cloned.1.call-done = bf16[1024,4096]{1,0:T(8,128)(2,1)} async-done(((bf16[1024,512]{1,0:T(8,128)(2,1)}), bf16[1024,4096]{1,0:T(8,128)(2,1)}) %all-gather.2.cloned.1.call-update) | async-done | bytes 8388624 | tf_op jit(solution)/shard_map/all_gather | solution.py:94
  168.3 9.5 %convolution_convert_fusion = bf16[512,4096]{1,0:T(8,128)(2,1)} fusion(bf16[512,1024]{0,1:T(8,128)(2,1)S(1)} %bitcast.193, bf16[1024,4096]{1,0:T(8,128)(2,1)} %all-gather.2.cloned.1.call-done), kind=kOutput, calls=%fused_computation.81 | convolution fusion | flops 4297064448 | bytes 13631488 | tf_op jit(solution)/shard_map/dot_general | solution.py:92
  177.8 48.5 %reduce-scatter.2.cloned.1.call-done = bf16[512,1024]{1,0:T(8,128)(2,1)} async-done(((bf16[512,4096]{1,0:T(8,128)(2,1)}), bf16[512,1024]{1,0:T(8,128)(2,1)}) %reduce-scatter.2.cloned.1.call-update) | async-done | bytes 1048592 | tf_op jit(solution)/shard_map/reduce_scatter | solution.py:97
  (36 shorter events, 1.0 us)
Async XLA Ops:
  6.5 161.8 %all-gather.2.cloned.1.call-start = ((), (), s32[]{:S(2)}) async-start(), calls=%async_computation.1 | async-start | bytes 9437184 | tf_op jit(solution)/shard_map/all_gather | solution.py:94
  7.3 219.1 %reduce-scatter.2.cloned.1.call-start = ((), (), s32[]{:S(2)}) async-start(), calls=%async_computation.2 | async-start | bytes 5242880 | tf_op jit(solution)/shard_map/reduce_scatter | solution.py:97
  9.5 90.7 %copy-start = (bf16[512,256]{0,1:T(8,128)(2,1)}, bf16[512,256]{0,1:T(8,128)(2,1)S(1)}, u32[]{:S(2)}) copy-start(bf16[512,256]{0,1:T(8,128)(2,1)S(1)} %copy.55) | copy-start | bytes 786436
  9.6 21.8 %collective-permute-start = (bf16[2,512,256]{1,2,0:T(8,128)(2,1)S(1)}, bf16[2,512,256]{1,2,0:T(8,128)(2,1)S(1)}, u32[]{:S(2)}, u32[]{:S(2)}) collective-permute-start(bf16[2,512,256]{1,2,0:T(8,128)(2,1)S(1)} %pad_maximum_fusion), channel_id=1, source_target_pairs={{0,4},{4,8},{8,12},{12,16},{16,20},{20,24},{24,28},{1,5},{5,9},{9,... | collective-permute-start | bytes 1572872 | tf_op jit(solution)/shard_map/ppermute | solution.py:16
  31.4 68.9 %copy-start.3 = (bf16[2,512,256]{1,2,0:T(8,128)(2,1)}, bf16[2,512,256]{1,2,0:T(8,128)(2,1)S(1)}, u32[]{:S(2)}) copy-start(bf16[2,512,256]{1,2,0:T(8,128)(2,1)S(1)} %collective-permute-done) | copy-start | bytes 1572868
  31.4 16.7 %collective-permute-start.1 = (bf16[2,512,256]{1,2,0:T(8,128)(2,1)S(1)}, bf16[2,512,256]{1,2,0:T(8,128)(2,1)S(1)}, u32[]{:S(2)}, u32[]{:S(2)}) collective-permute-start(bf16[2,512,256]{1,2,0:T(8,128)(2,1)S(1)} %collective-permute-done), channel_id=1, source_target_pairs={{0,4},{4,8},{8,12},{12,16},{16,20},{20,24},{24,28},{1,5},{5,9},{9,... | collective-permute-start | bytes 1572872 | tf_op jit(solution)/shard_map/ppermute | solution.py:16
  48.1 52.2 %copy-start.2 = (bf16[2,512,256]{1,2,0:T(8,128)(2,1)}, bf16[2,512,256]{1,2,0:T(8,128)(2,1)S(1)}, u32[]{:S(2)}) copy-start(bf16[2,512,256]{1,2,0:T(8,128)(2,1)S(1)} %collective-permute-done.1) | copy-start | bytes 1572868
  48.1 18.8 %collective-permute-start.2 = (bf16[2,512,256]{1,2,0:T(8,128)(2,1)S(1)}, bf16[2,512,256]{1,2,0:T(8,128)(2,1)}, u32[]{:S(2)}, u32[]{:S(2)}) collective-permute-start(bf16[2,512,256]{1,2,0:T(8,128)(2,1)S(1)} %collective-permute-done.1), channel_id=1, source_target_pairs={{0,4},{4,8},{8,12},{12,16},{16,20},{20,24},{24,28},{1,5},{5,9},{9,... | collective-permute-start | bytes 1572872 | tf_op jit(solution)/shard_map/ppermute | solution.py:16
  66.9 43.8 %collective-permute-start.3 = (bf16[2,512,256]{1,2,0:T(8,128)(2,1)}, bf16[2,512,256]{1,2,0:T(8,128)(2,1)}, u32[]{:S(2)}, u32[]{:S(2)}) collective-permute-start(bf16[2,512,256]{1,2,0:T(8,128)(2,1)} %collective-permute-done.2), channel_id=1, source_target_pairs={{0,4},{4,8},{8,12},{12,16},{16,20},{20,24},{24,28},{1,5},{5,9},{9,... | collective-permute-start | bytes 1572872 | tf_op jit(solution)/shard_map/ppermute | solution.py:16
  100.7 3.7 %copy-start.1 = (bf16[512,2,128]{0,2,1:T(8,128)(2,1)S(1)}, bf16[512,2,128]{0,2,1:T(8,128)(2,1)}, u32[]{:S(2)}) copy-start(bf16[512,2,128]{0,2,1:T(8,128)(2,1)} %get-tuple-element.480) | copy-start | bytes 786436 | tf_op jit(solution)/shard_map/while/body/eval_jaxpr/cond
Sparse Core Ops, SparseCore 0:
  9.4 158.9 all-gather.1
  178.0 48.3 reduce-scatter.1
where the time goes:
time: 234 us; the launch traced here: 233 us
  waiting for transfers between devices  137 us (59%)
  starting transfers between devices  40.7 us (17%)
  between operations  22.6 us (10%)
  matrix products  14.7 us (6%)
  local copies, waits for them, and re-layouts  12.2 us (5%)
  other arithmetic  5.23 us (2%)
    all_gather x1, waiting for transfers between devices, body(): lax.all_gather(out_weight, 'seq', axis=1, tiled=True)  53.9 us
    reduce_scatter x1, waiting for transfers between devices, body(): lax.psum_scatter(partial_terms.astype(jnp.bfloat16), 'head', scatter_dime...  48.5 us
    ppermute x4, starting transfers between devices, from_behind(): return lax.ppermute(block, axis, route)  40.7 us
    ppermute x4, waiting for transfers between devices, from_behind(): return lax.ppermute(block, axis, route)  34 us
    dot_general x1, matrix products, body(): jnp.dot(attn, lax.all_gather(out_weight, 'seq', axis=1, tiled=True), pref...  9.46 us
  transfers between devices with their start and end apart: 6, of which 5 were waited for; matrix products, arithmetic and copies ran while one was open for 10% of the time, Pallas kernels for 0%

commit v1 on v0

--- a/solution.py
+++ b/solution.py
@@ -91,7 +91,9 @@
     attn = jnp.transpose(attn, (2, 0, 1, 3)).reshape(local_rows, kv_local * group_size * DH)
     partial_terms = jnp.dot(
         attn,
-        lax.all_gather(out_weight, "seq", axis=1, tiled=True),
+        jnp.concatenate(
+            lax.all_to_all(jnp.stack([out_weight] * lax.axis_size("seq")), "seq", 0, 0), axis=1
+        ),
         preferred_element_type=jnp.float32,
     )
     return lax.psum_scatter(

time: 234 us -> 377 us (1.61); the launches traced: 233 us -> 370 us
  starting transfers between devices: 40.7 us -> 137 us
  waiting for transfers between devices: 137 us -> 166 us
  loops' own time: 0.52 us -> 7.98 us
    ppermute x4, starting transfers between devices: 40.7 us -> 130 us  [from_behind(): return lax.ppermute(block, axis, route)]
    ppermute x4, waiting for transfers between devices: 34 us -> 93.5 us  [from_behind(): return lax.ppermute(block, axis, route)]
    all_gather x1 -> x0, waiting for transfers between devices: 53.9 us -> none  [body(): lax.all_gather(out_weight, 'seq', axis=1, tiled=True)]
    reduce_scatter x1, waiting for transfers between devices: 48.5 us -> 72.5 us  [body(): lax.psum_scatter(partial_terms.astype(jnp.bfloat16), 'head', scatter_dime...]
    another operation x5, loops' own time: 0.52 us -> 7.98 us  [one_block(): return (lax.cond(needed, update, unchanged, state), None)]
    all_to_all x0 -> x1, starting transfers between devices: none -> 7.45 us  [body(): lax.all_to_all(jnp.stack([out_weight] * lax.axis_size('seq')), 'seq', 0, 0)]
  transfers between devices with their start and end apart: 6 -> 6, of which waited for: 5 -> 4; matrix products, arithmetic and copies ran while one was open for 10% -> 5% of each run, Pallas kernels for 0% -> 0%
where the time goes in v1:
time: 377 us; the launch traced here: 370 us
  waiting for transfers between devices  166 us (44%)
  starting transfers between devices  137 us (36%)
  between operations  22.9 us (6%)
  local copies, waits for them, and re-layouts  15.9 us (4%)
  matrix products  14.9 us (4%)
  loops' own time  7.98 us (2%)
  other arithmetic  4.56 us (1%)
    ppermute x4, starting transfers between devices, from_behind(): return lax.ppermute(block, axis, route)  130 us
    ppermute x4, waiting for transfers between devices, from_behind(): return lax.ppermute(block, axis, route)  93.5 us
    reduce_scatter x1, waiting for transfers between devices, body(): lax.psum_scatter(partial_terms.astype(jnp.bfloat16), 'head', scatter_dime...  72.5 us
    dot_general x1, matrix products, body(): jnp.dot(attn, jnp.concatenate(lax.all_to_all(jnp.stack([out_weight] * lax...  9.63 us
    another operation x5, loops' own time, one_block(): return (lax.cond(needed, update, unchanged, state), None)  7.98 us
  transfers between devices with their start and end apart: 6, of which 4 were waited for; matrix products, arithmetic and copies ran while one was open for 5% of the time, Pallas kernels for 0%

profile of v1, /device:TPU:0, one launch (start us, length us, event | category | flops | bytes accessed | tf_op | source)
XLA Modules:
  0.0 369.6 jit_solution(1898710234335323139)
XLA Ops:
  6.5 1.5 copy.71
  8.0 4.3 %stack.11 = bf16[8,1024,512]{1,2,0:T(8,128)(2,1)} broadcast(bf16[1024,512]{0,1:T(8,128)(2,1)S(1)} %copy.71), dimensions={1,2} | broadcast | bytes 9437184 | tf_op jit(solution)/shard_map/stack | solution.py:95
  12.3 7.5 %all-to-all-start = ((bf16[8,1024,512]{1,2,0:T(8,128)(2,1)}), bf16[8,1024,512]{1,2,0:T(8,128)(2,1)}, u32[]{:S(2)}, u32[]{:S(2)}) async-start(bf16[8,1024,512]{1,2,0:T(8,128)(2,1)} %stack.11), calls=%async_computation | async-start | bytes 16777216 | tf_op jit(solution)/shard_map/all_to_all | solution.py:95
  20.0 0.1 copy.56
  20.2 3.9 %collective-permute-start = (bf16[2,512,256]{1,2,0:T(8,128)(2,1)S(1)}, bf16[2,512,256]{1,2,0:T(8,128)(2,1)S(1)}, u32[]{:S(2)}, u32[]{:S(2)}) collective-permute-start(bf16[2,512,256]{1,2,0:T(8,128)(2,1)S(1)} %pad_maximum_fusion), channel_id=1, source_target_pairs={{0,4},{4,8},{8,12},{12,16},{16,20},{20,24},{24,28},{1,5},{5,9},{9,... | collective-permute-start | bytes 1572872 | tf_op jit(solution)/shard_map/ppermute | solution.py:16
  24.4 75.4 %collective-permute-done = bf16[2,512,256]{1,2,0:T(8,128)(2,1)S(1)} collective-permute-done((bf16[2,512,256]{1,2,0:T(8,128)(2,1)S(1)}, bf16[2,512,256]{1,2,0:T(8,128)(2,1)S(1)}, u32[]{:S(2)}, u32[]{:S(2)}) %collective-permute-start) | collective-permute-done | bytes 524320 | tf_op jit(solution)/shard_map/ppermute | solution.py:16
  99.8 79.3 %collective-permute-start.1 = (bf16[2,512,256]{1,2,0:T(8,128)(2,1)S(1)}, bf16[2,512,256]{1,2,0:T(8,128)(2,1)S(1)}, u32[]{:S(2)}, u32[]{:S(2)}) collective-permute-start(bf16[2,512,256]{1,2,0:T(8,128)(2,1)S(1)} %collective-permute-done), channel_id=1, source_target_pairs={{0,4},{4,8},{8,12},{12,16},{16,20},{20,24},{24,28},{1,5},{5,9},{9,... | collective-permute-start | bytes 1572872 | tf_op jit(solution)/shard_map/ppermute | solution.py:16
  179.3 11.3 %collective-permute-done.1 = bf16[2,512,256]{1,2,0:T(8,128)(2,1)S(1)} collective-permute-done((bf16[2,512,256]{1,2,0:T(8,128)(2,1)S(1)}, bf16[2,512,256]{1,2,0:T(8,128)(2,1)S(1)}, u32[]{:S(2)}, u32[]{:S(2)}) %collective-permute-start.1) | collective-permute-done | bytes 524320 | tf_op jit(solution)/shard_map/ppermute | solution.py:16
  190.6 13.0 %collective-permute-start.2 = (bf16[2,512,256]{1,2,0:T(8,128)(2,1)S(1)}, bf16[2,512,256]{1,2,0:T(8,128)(2,1)}, u32[]{:S(2)}, u32[]{:S(2)}) collective-permute-start(bf16[2,512,256]{1,2,0:T(8,128)(2,1)S(1)} %collective-permute-done.1), channel_id=1, source_target_pairs={{0,4},{4,8},{8,12},{12,16},{16,20},{20,24},{24,28},{1,5},{5,9},{9,... | collective-permute-start | bytes 1572872 | tf_op jit(solution)/shard_map/ppermute | solution.py:16
  203.7 6.9 %collective-permute-done.2 = bf16[2,512,256]{1,2,0:T(8,128)(2,1)} collective-permute-done((bf16[2,512,256]{1,2,0:T(8,128)(2,1)S(1)}, bf16[2,512,256]{1,2,0:T(8,128)(2,1)}, u32[]{:S(2)}, u32[]{:S(2)}) %collective-permute-start.2) | collective-permute-done | bytes 524320 | tf_op jit(solution)/shard_map/ppermute | solution.py:16
  210.5 33.5 %collective-permute-start.3 = (bf16[2,512,256]{1,2,0:T(8,128)(2,1)}, bf16[2,512,256]{1,2,0:T(8,128)(2,1)}, u32[]{:S(2)}, u32[]{:S(2)}) collective-permute-start(bf16[2,512,256]{1,2,0:T(8,128)(2,1)} %collective-permute-done.2), channel_id=1, source_target_pairs={{0,4},{4,8},{8,12},{12,16},{16,20},{20,24},{24,28},{1,5},{5,9},{9,... | collective-permute-start | bytes 1572872 | tf_op jit(solution)/shard_map/ppermute | solution.py:16
  244.0 0.7 fusion.68
  244.6 0.6 slice.72
  247.9 0.6 slice.76
  248.6 0.6 slice.77
  252.9 0.7 slice.75
  254.8 0.6 slice.73
  256.8 0.5 copy.55
  257.5 7.7 %conditional.5 = ((f32[2,4,512]{2,1,0:T(4,128)S(1)}, f32[2,4,512]{2,1,0:T(4,128)S(1)}, f32[2,4,512,128]{3,2,1,0:T(8,128)S(1)})) conditional(s32[]{:T(128)} %convert_element_type.72, (f32[2,4,512]{2,1,0:T(4,128)S(1)}, f32[2,4,512]{2,1,0:T(4,128)S(1)}, f32[2,4,512,128]{3,2,1,0:T(8,128)S(1)}) %tuple.52, (s32[512]{0:T(512)S(1)}, s32[512]{0:T(512)S(1)}, ...), branch_computations={%region_6.7_spmd, %region_7.10_spmd} | conditional | flops 1102848000 | bytes 33296444 | solution.py:74
  257.5 0.3 compare_and_fusion
  257.8 1.6 fusion
  259.4 2.0 fusion.2
  261.5 3.6 multiply_add_fusion
  265.2 1.8 fusion.67
  267.0 0.4 conditional.6
  267.4 1.8 fusion.66
  269.2 6.6 %conditional.8 = ((f32[2,4,512]{2,1,0:T(4,128)S(1)}, f32[2,4,512]{2,1,0:T(4,128)S(1)}, f32[2,4,512,128]{3,2,1,0:T(8,128)S(1)})) conditional(s32[]{:T(128)} %convert_element_type.67, (f32[2,4,512]{2,1,0:T(4,128)S(1)}, f32[2,4,512]{2,1,0:T(4,128)S(1)}, f32[2,4,512,128]{3,2,1,0:T(8,128)S(1)}) %get-tuple-element.601, (s32[512]{0:T(512)S(1)}, ...), branch_computations={%region_18.19_spmd, %region_19.22_spmd} | conditional | flops 1102848512 | bytes 33304612 | solution.py:74
  275.8 2.7 conditional.9
  275.8 1.8 copy.112
  278.5 1.9 divide_convert_fusion
  280.4 9.6 %convolution_convert_fusion = bf16[512,4096]{1,0:T(8,128)(2,1)} fusion(bf16[512,1024]{0,1:T(8,128)(2,1)S(1)} %bitcast.196, bf16[1024,4096]{0,1:T(8,128)(2,1)} %bitcast.38), kind=kOutput, calls=%fused_computation.81 | convolution fusion | flops 4297064448 | bytes 13631488 | tf_op jit(solution)/shard_map/dot_general | solution.py:92
  290.0 72.5 %reduce-scatter.2.cloned.1.call-done = bf16[512,1024]{1,0:T(8,128)(2,1)} async-done(((bf16[512,4096]{1,0:T(8,128)(2,1)}), bf16[512,1024]{1,0:T(8,128)(2,1)}) %reduce-scatter.2.cloned.1.call-update) | async-done | bytes 1048592 | tf_op jit(solution)/shard_map/reduce_scatter | solution.py:99
  (45 shorter events, 0.8 us)
Async XLA Ops:
  12.3 7.5 %copy-start.5 = (bf16[512,256]{1,0:T(8,128)(2,1)S(1)}, bf16[512,256]{1,0:T(8,128)(2,1)}, u32[]{:S(2)}) copy-start(bf16[512,256]{1,0:T(8,128)(2,1)} %param.16) | copy-start | bytes 786436
  12.3 7.7 %copy-start.6 = (bf16[512,256]{1,0:T(8,128)(2,1)S(1)}, bf16[512,256]{1,0:T(8,128)(2,1)}, u32[]{:S(2)}) copy-start(bf16[512,256]{1,0:T(8,128)(2,1)} %param.17) | copy-start | bytes 786436
  12.3 11.8 %copy-start.9 = (s32[16]{0:T(128)S(1)}, s32[16]{0:T(128)}, u32[]{:S(2)}) copy-start(s32[16]{0:T(128)} %param.18) | copy-start | bytes 196
  12.3 244.4 %copy-start = (bf16[512,1024]{1,0:T(8,128)(2,1)S(1)}, bf16[512,1024]{1,0:T(8,128)(2,1)}, u32[]{:S(2)}) copy-start(bf16[512,1024]{1,0:T(8,128)(2,1)} %param.15) | copy-start | bytes 3145732
  12.3 268.0 %all-to-all-start = ((bf16[8,1024,512]{1,2,0:T(8,128)(2,1)}), bf16[8,1024,512]{1,2,0:T(8,128)(2,1)}, u32[]{:S(2)}, u32[]{:S(2)}) async-start(bf16[8,1024,512]{1,2,0:T(8,128)(2,1)} %stack.11), calls=%async_computation | async-start | bytes 16777216 | tf_op jit(solution)/shard_map/all_to_all | solution.py:95
  19.8 342.8 %reduce-scatter.2.cloned.1.call-start = ((), (), s32[]{:S(2)}) async-start(), calls=%async_computation.2 | async-start | bytes 5242880 | tf_op jit(solution)/shard_map/reduce_scatter | solution.py:99
  20.1 237.2 %copy-start.1 = (bf16[512,256]{0,1:T(8,128)(2,1)}, bf16[512,256]{0,1:T(8,128)(2,1)S(1)}, u32[]{:S(2)}) copy-start(bf16[512,256]{0,1:T(8,128)(2,1)S(1)} %copy.56) | copy-start | bytes 786436
  20.2 79.6 %collective-permute-start = (bf16[2,512,256]{1,2,0:T(8,128)(2,1)S(1)}, bf16[2,512,256]{1,2,0:T(8,128)(2,1)S(1)}, u32[]{:S(2)}, u32[]{:S(2)}) collective-permute-start(bf16[2,512,256]{1,2,0:T(8,128)(2,1)S(1)} %pad_maximum_fusion), channel_id=1, source_target_pairs={{0,4},{4,8},{8,12},{12,16},{16,20},{20,24},{24,28},{1,5},{5,9},{9,... | collective-permute-start | bytes 1572872 | tf_op jit(solution)/shard_map/ppermute | solution.py:16
  99.8 156.9 %copy-start.4 = (bf16[2,512,256]{1,2,0:T(8,128)(2,1)}, bf16[2,512,256]{1,2,0:T(8,128)(2,1)S(1)}, u32[]{:S(2)}) copy-start(bf16[2,512,256]{1,2,0:T(8,128)(2,1)S(1)} %collective-permute-done) | copy-start | bytes 1572868
  99.8 90.8 %collective-permute-start.1 = (bf16[2,512,256]{1,2,0:T(8,128)(2,1)S(1)}, bf16[2,512,256]{1,2,0:T(8,128)(2,1)S(1)}, u32[]{:S(2)}, u32[]{:S(2)}) collective-permute-start(bf16[2,512,256]{1,2,0:T(8,128)(2,1)S(1)} %collective-permute-done), channel_id=1, source_target_pairs={{0,4},{4,8},{8,12},{12,16},{16,20},{20,24},{24,28},{1,5},{5,9},{9,... | collective-permute-start | bytes 1572872 | tf_op jit(solution)/shard_map/ppermute | solution.py:16
  190.6 66.7 %copy-start.3 = (bf16[2,512,256]{1,2,0:T(8,128)(2,1)}, bf16[2,512,256]{1,2,0:T(8,128)(2,1)S(1)}, u32[]{:S(2)}) copy-start(bf16[2,512,256]{1,2,0:T(8,128)(2,1)S(1)} %collective-permute-done.1) | copy-start | bytes 1572868
  190.6 19.9 %collective-permute-start.2 = (bf16[2,512,256]{1,2,0:T(8,128)(2,1)S(1)}, bf16[2,512,256]{1,2,0:T(8,128)(2,1)}, u32[]{:S(2)}, u32[]{:S(2)}) collective-permute-start(bf16[2,512,256]{1,2,0:T(8,128)(2,1)S(1)} %collective-permute-done.1), channel_id=1, source_target_pairs={{0,4},{4,8},{8,12},{12,16},{16,20},{20,24},{24,28},{1,5},{5,9},{9,... | collective-permute-start | bytes 1572872 | tf_op jit(solution)/shard_map/ppermute | solution.py:16
  210.5 65.3 %collective-permute-start.3 = (bf16[2,512,256]{1,2,0:T(8,128)(2,1)}, bf16[2,512,256]{1,2,0:T(8,128)(2,1)}, u32[]{:S(2)}, u32[]{:S(2)}) collective-permute-start(bf16[2,512,256]{1,2,0:T(8,128)(2,1)} %collective-permute-done.2), channel_id=1, source_target_pairs={{0,4},{4,8},{8,12},{12,16},{16,20},{20,24},{24,28},{1,5},{5,9},{9,... | collective-permute-start | bytes 1572872 | tf_op jit(solution)/shard_map/ppermute | solution.py:16
  257.8 3.7 %copy-start.2 = (bf16[512,2,128]{0,2,1:T(8,128)(2,1)S(1)}, bf16[512,2,128]{0,2,1:T(8,128)(2,1)}, u32[]{:S(2)}) copy-start(bf16[512,2,128]{0,2,1:T(8,128)(2,1)} %get-tuple-element.480) | copy-start | bytes 786436 | tf_op jit(solution)/shard_map/while/body/eval_jaxpr/cond
Sparse Core Ops, SparseCore 0:
  290.2 72.3 reduce-scatter.1
